TPU v7x, 256 devices: a whole 4x4x8 slice. The times are simulated.
256 devices in a mesh: dp: 16 (over y, x), expert: 8 (over z), tensor: 2 (over core).
Axes of the slice: x: 4, y: 4, z: 8, core: 2. Of those that a mesh axis runs over, the one named last changes fastest.
Arguments:
- tokens: bfloat16 [2048, 4096], P(('dp', 'expert'), 'tensor'), may hold values from -6 to 6
- target: bfloat16 [2048, 4096], P(('dp', 'expert'), 'tensor'), may hold values from -4 to 4
- router: bfloat16 [4096, 8], P('tensor'), may hold values from -1 to 1
- w_gate: bfloat16 [8, 4096, 14336], P('expert', None, ('dp', 'tensor')), may hold values from -1 to 1
- w_up: bfloat16 [8, 4096, 14336], P('expert', None, ('dp', 'tensor')), may hold values from -1 to 1
- w_down: bfloat16 [8, 14336, 4096], P('expert', ('dp', 'tensor')), may hold values from -1 to 1
- expert_ids: int32 [2048, 2], P(('dp', 'expert')), may hold values from 0 to 7, as said below
- lengths: int32 [64], replicated, may hold values from 1 to 128, 2048 in all
- bench_ids: int32 [64], replicated, may hold values from 0 to 15
Outputs:
- mixed: bfloat16 [2048, 4096], P(('dp', 'expert'), 'tensor')
- bench_loss: float32 [16], replicated
- counts: int32 [16], replicated
Inputs may be any that keep to these rules, and one draw needn't show every extreme that they name: `expert_ids`: each row names two different experts; among the 16 rows of one device no expert is named by more than 8 rows; for each index of dp, one expert is named by exactly 8 rows of every device of that index. The lengths sum to 2048.
All inputs are finite; a program needn't handle non-finite values.
Results may differ from a plain program's by a relative error of at most 0.0085.
Values may be sent and summed in bfloat16 or wider, within the bound.
A program may use at most 128 MiB of HBM per device.

v0:
```python
import jax
import jax.numpy as jnp
from jax import lax
from jax.sharding import Mesh
from jax.sharding import PartitionSpec as P

D = 4096
NB = 16
CAP = 8
DP = ("dp_0", "dp_1")
DP_EXPERT = ("dp_0", "dp_1", "expert")
DP_EXPERT_TENSOR = ("dp_0", "dp_1", "expert", "tensor")
DP_TENSOR = ("dp_0", "dp_1", "tensor")


def cut_along(shard, dim, size):
    before, after = (shard.shape[:dim], shard.shape[dim + 1 :])
    return jnp.moveaxis(shard.reshape(*before, size, -1, *after), dim, 0)


def sent_and_summed(shard, axis, dim):
    pieces = cut_along(shard, dim, lax.axis_size(axis))
    arrived = lax.all_to_all(pieces, axis, split_axis=0, concat_axis=0, tiled=True)
    return arrived.sum(axis=0)


def one_axis_at_a_time(shard, axes):
    for axis in axes:
        shard = lax.psum(shard, axis)
    return shard


def per_device(tokens, target, router, w_gate, w_up, w_down, expert_ids, lengths, bench_ids):
    tensor_count = lax.axis_size("tensor")
    local_tokens = tokens.shape[0]
    experts = router.shape[1]
    half_cap = CAP // tensor_count
    slot_rows = tensor_count * experts * half_cap
    partial_value = jnp.dot(tokens, router, preferred_element_type=jnp.float32)
    logits = lax.psum(partial_value, "tensor")
    chosen = expert_ids[:, :, None] == jnp.arange(experts, dtype=jnp.int32)[None, None, :]
    picked = jnp.sum(jnp.where(chosen, logits[:, None, :], jnp.float32(0.0)), axis=2)
    gates = jnp.stack(
        [jax.nn.sigmoid(picked[:, 0] - picked[:, 1]), jax.nn.sigmoid(picked[:, 1] - picked[:, 0])],
        axis=1,
    )
    marks = chosen.reshape(local_tokens * 2, experts).astype(jnp.int32)
    before = jnp.cumsum(marks, axis=0) - marks
    slot = jnp.sum(before * marks, axis=1)
    flat_ids = expert_ids.reshape(local_tokens * 2)
    target_row = slot // half_cap * (experts * half_cap) + flat_ids * half_cap + slot % half_cap
    placing = (target_row[None, :] == jnp.arange(slot_rows, dtype=jnp.int32)[:, None]).reshape(
        slot_rows, local_tokens, 2
    )
    dispatch_map = jnp.any(placing, axis=2).astype(jnp.bfloat16)
    outgoing = jnp.dot(dispatch_map, tokens, preferred_element_type=jnp.float32).astype(
        jnp.bfloat16
    )
    outgoing = outgoing.reshape(tensor_count, experts, half_cap, tokens.shape[1])
    arrived = lax.all_to_all(outgoing, "expert", split_axis=1, concat_axis=1, tiled=True)
    whole = lax.all_gather(arrived, "tensor", axis=3, tiled=True)
    whole = whole.reshape(1, slot_rows, D)
    every_row = lax.all_gather(whole, DP, axis=0, tiled=True).reshape(-1, D)
    gate_w = w_gate[0]
    up_w = w_up[0]
    down_w = w_down[0]
    gate = jnp.dot(every_row, gate_w, preferred_element_type=jnp.float32)
    up = jnp.dot(every_row, up_w, preferred_element_type=jnp.float32)
    hidden = (jax.nn.silu(gate) * up).astype(jnp.bfloat16)
    summed = lax.psum_scatter(
        jnp.dot(hidden, down_w, preferred_element_type=jnp.float32),
        DP,
        scatter_dimension=0,
        tiled=True,
    )
    summed = sent_and_summed(summed, "tensor", 1)
    results = summed.astype(jnp.bfloat16).reshape(
        tensor_count, experts, half_cap, D // tensor_count
    )
    returned = lax.all_to_all(results, "expert", split_axis=1, concat_axis=1, tiled=True)
    weights = jnp.einsum("rtk,tk->tr", placing.astype(jnp.float32), gates)
    flat_back = returned.reshape(slot_rows, -1).astype(jnp.float32)
    mixed = jnp.dot(weights, flat_back, precision=lax.Precision.HIGHEST).astype(jnp.bfloat16)
    first_index = lax.axis_index(DP_EXPERT) * local_tokens
    position = first_index + jnp.arange(local_tokens, dtype=jnp.int32)
    ends = jnp.cumsum(lengths)
    starts = ends - lengths
    inside = ((position[:, None] >= starts[None, :]) & (position[:, None] < ends[None, :])).astype(
        jnp.float32
    )
    closing = jnp.any((position + 1)[:, None] == ends[None, :], axis=1)
    scored = jnp.where(closing, jnp.float32(0.0), jnp.float32(1.0))
    bench_table = bench_ids[:, None] == jnp.arange(NB, dtype=jnp.int32)[None, :]
    bench_of = jnp.dot(inside, bench_table.astype(jnp.float32), precision=lax.Precision.HIGHEST)
    diff = mixed.astype(jnp.float32) - target.astype(jnp.float32)
    token_part = jnp.sum(diff * diff, axis=1) / D
    local_sums = jnp.dot(scored * token_part, bench_of, precision=lax.Precision.HIGHEST)
    loss_sum = one_axis_at_a_time(local_sums, DP_EXPERT_TENSOR)
    counts = jnp.sum(jnp.where(bench_table, (lengths - 1)[:, None], 0), axis=0)
    bench_loss = loss_sum / jnp.maximum(counts, 1).astype(jnp.float32)
    return (mixed, bench_loss, counts)


def solution(mesh):
    split = Mesh(
        mesh.devices.reshape(4, 4, mesh.shape["expert"], mesh.shape["tensor"]),
        ("dp_0", "dp_1", "expert", "tensor"),
    )
    in_specs = (
        P(DP_EXPERT, "tensor"),
        P(DP_EXPERT, "tensor"),
        P("tensor", None),
        P("expert", None, DP_TENSOR),
        P("expert", None, DP_TENSOR),
        P("expert", DP_TENSOR, None),
        P(DP_EXPERT, None),
        P(),
        P(),
    )
    out_specs = (P(DP_EXPERT, "tensor"), P(), P())
    return jax.shard_map(
        per_device, mesh=split, in_specs=in_specs, out_specs=out_specs, check_vma=False
    )
```

profile of v0, /device:TPU:1, one launch (start us, length us, event | category | flops | bytes accessed | tf_op | source)
XLA Modules:
  0.0 317.1 jit_solution(9953797493856227956)
XLA Ops:
  7.2 0.8 copy.53
  8.2 0.2 select_reduce_fusion
  8.6 0.7 fusion.22
  9.4 0.3 convolution_convert_fusion
  9.8 19.3 %all_to_all.15 = bf16[2,8,4,2048]{3,2,0,1:T(4,128)(2,1)S(1)} all-to-all(bf16[2,8,4,2048]{3,2,0,1:T(4,128)(2,1)S(1)} %copy.58), channel_id=1, replica_groups=mesh['dp_0'=4,'dp_1'=4,'expert'=8,'tensor'=2] {'expert'}, dimensions={1} | all-to-all | bytes 524288 | tf_op jit(solution)/shard_map/all_to_all | solution.py:60
  29.2 4.1 %all_gather.6 = bf16[2,8,4,4096]{3,2,0,1:T(4,128)(2,1)S(1)} all-gather(bf16[2,8,4,2048]{3,2,0,1:T(4,128)(2,1)S(1)} %all_to_all.15), channel_id=1, replica_groups=mesh['dp_0'=4,'dp_1'=4,'expert'=8,'tensor'=2] {'tensor'}, dimensions={3}, use_global_device_ids=true | all-gather | bytes 786432 | tf_op jit(solution)/shard_map/all_gather | solution.py:61
  33.3 0.2 copy.59
  33.5 0.9 reshape.109
  34.5 71.8 %all-gather.2.cloned.1.call-done = bf16[16,64,4096]{2,1,0:T(8,128)(2,1)} async-done(((bf16[1,64,4096]{2,1,0:T(8,128)(2,1)}), bf16[16,64,4096]{2,1,0:T(8,128)(2,1)}) %all-gather.2.cloned.1.call-update) | async-done | bytes 8388624 | tf_op jit(solution)/shard_map/all_gather | solution.py:63
  106.3 7.5 %fusion.4 = f32[1024,448]{0,1:T(8,128)S(1)} fusion(bf16[1024,4096]{1,0:T(8,128)(2,1)} %bitcast.45, bf16[1,4096,448]{1,2,0:T(8,128)(2,1)} %param.12), kind=kOutput, calls=%fused_computation.4 | convolution fusion | flops 3758096384 | bytes 13893632 | tf_op jit(solution)/shard_map/dot_general | solution.py:67
  113.8 16.5 %fusion = f32[1024,4096]{1,0:T(8,128)} fusion(bf16[1,448,4096]{2,1,0:T(8,128)(2,1)} %param.14, f32[1024,448]{0,1:T(8,128)S(1)} %fusion.4, bf16[1024,4096]{1,0:T(8,128)(2,1)} %bitcast.46, bf16[1,4096,448]{1,2,0:T(8,128)(2,1)} %param.13), kind=kOutput, calls=%fused_computation | convolution fusion | flops 7518945280 | bytes 34340864 | tf_op jit(solution)/shard_map/dot_general | solution.py:71
  130.4 0.6 copy-done.4
  131.2 0.1 reduce
  131.3 0.1 fusion.35
  131.4 3.0 psum.35
  134.4 0.1 select_reduce_fusion.1
  134.5 0.2 compare_reduce_fusion
  134.7 111.3 %reduce-scatter.2.cloned.1.call-done = f32[64,4096]{1,0:T(8,128)} async-done(((f32[1024,4096]{1,0:T(8,128)}), f32[64,4096]{1,0:T(8,128)}) %reduce-scatter.2.cloned.1.call-update) | async-done | bytes 1048592 | tf_op jit(solution)/shard_map/reduce_scatter | solution.py:70
  246.0 1.3 copy.71
  247.3 5.1 %all_to_all.16 = f32[2,64,2048]{2,1,0:T(8,128)S(1)} all-to-all(f32[2,64,2048]{2,1,0:T(8,128)S(1)} %bitcast.41), channel_id=1, replica_groups=mesh['dp_0'=4,'dp_1'=4,'expert'=8,'tensor'=2] {'tensor'}, dimensions={0} | all-to-all | bytes 2097152 | tf_op jit(solution)/shard_map/all_to_all | solution.py:23
  252.6 0.8 copy.61
  253.4 6.8 %all-to-all-start.2 = ((bf16[2,8,4,2048]{3,2,0,1:T(4,128)(2,1)}), bf16[2,8,4,2048]{3,2,0,1:T(4,128)(2,1)S(1)}, u32[]{:S(2)}, u32[]{:S(2)}) async-start(bf16[2,8,4,2048]{3,2,0,1:T(4,128)(2,1)} %copy.61), calls=%async_computation.3 | async-start | bytes 524288 | tf_op jit(solution)/shard_map/all_to_all | solution.py:80
  260.3 0.2 fusion.14
  260.5 0.1 fusion.11
  260.6 10.7 %all-to-all-done.2 = bf16[2,8,4,2048]{3,2,0,1:T(4,128)(2,1)S(1)} async-done(((bf16[2,8,4,2048]{3,2,0,1:T(4,128)(2,1)}), bf16[2,8,4,2048]{3,2,0,1:T(4,128)(2,1)S(1)}, u32[]{:S(2)}, u32[]{:S(2)}) %all-to-all-start.2) | async-done | bytes 262176 | tf_op jit(solution)/shard_map/all_to_all | solution.py:80
  271.5 1.0 multiply_reduce_fusion
  272.4 0.1 convolution_bitcast_fusion
  272.6 8.0 %psum.36 = f32[16]{0:T(128)S(1)} all-reduce(f32[16]{0:T(128)S(1)} %convolution_bitcast_fusion), channel_id=1, replica_groups=mesh['dp_0'=4,'dp_1'=4,'expert'=8,'tensor'=2] {'dp_0'}, use_global_device_ids=true, to_apply=%region_10.11 | all-reduce | flops 16 | bytes 128 | tf_op jit(solution)/shard_map/psum | solution.py:29
  280.5 6.7 %psum.37 = f32[16]{0:T(128)S(1)} all-reduce(f32[16]{0:T(128)S(1)} %psum.36), channel_id=1, replica_groups=mesh['dp_0'=4,'dp_1'=4,'expert'=8,'tensor'=2] {'dp_1'}, use_global_device_ids=true, to_apply=%region_11.12 | all-reduce | flops 16 | bytes 128 | tf_op jit(solution)/shard_map/psum | solution.py:29
  287.2 10.7 %psum.38 = f32[16]{0:T(128)S(1)} all-reduce(f32[16]{0:T(128)S(1)} %psum.37), channel_id=1, replica_groups=mesh['dp_0'=4,'dp_1'=4,'expert'=8,'tensor'=2] {'expert'}, use_global_device_ids=true, to_apply=%region_12.13 | all-reduce | flops 16 | bytes 128 | tf_op jit(solution)/shard_map/psum | solution.py:29
  297.9 11.9 %psum.39 = f32[16]{0:T(128)S(1)} all-reduce(f32[16]{0:T(128)S(1)} %psum.38), channel_id=1, replica_groups=mesh['dp_0'=4,'dp_1'=4,'expert'=8,'tensor'=2] {'tensor'}, use_global_device_ids=true, to_apply=%region_13.14 | all-reduce | flops 16 | bytes 128 | tf_op jit(solution)/shard_map/psum | solution.py:29
  309.8 0.5 convert_divide_fusion
  (37 shorter events, 1.5 us)
Async XLA Ops:
  7.2 2.2 copy-start
  7.2 99.1 %all-gather.2.cloned.1.call-start = ((), (), s32[]{:S(2)}) async-start(), calls=%async_computation.4 | async-start | bytes 8912896 | tf_op jit(solution)/shard_map/all_gather | solution.py:63
  34.4 211.6 %reduce-scatter.2.cloned.1.call-start = ((), (), s32[]{:S(2)}) async-start(), calls=%async_computation.5 | async-start | bytes 17825792 | tf_op jit(solution)/shard_map/reduce_scatter | solution.py:70
  130.3 0.7 copy-start.4
  130.3 1.0 copy-start.2
  130.3 4.1 %copy-start.5 = (s32[64]{0:T(128)S(1)}, s32[64]{0:T(128)}, u32[]{:S(2)}) copy-start(s32[64]{0:T(128)} %param.17) | copy-start | bytes 772
  130.3 4.2 %copy-start.3 = (s32[16,2]{0,1:T(2,128)S(1)}, s32[16,2]{0,1:T(2,128)}, u32[]{:S(2)}) copy-start(s32[16,2]{0,1:T(2,128)} %param.15) | copy-start | bytes 388
  134.5 175.3 %copy-start.6 = (s32[16]{0:T(128)}, s32[16]{0:T(128)S(1)}, u32[]{:S(2)}) copy-start(s32[16]{0:T(128)S(1)} %select_reduce_fusion.1) | copy-start | bytes 196
  246.0 25.5 %copy-start.1 = (bf16[16,2048]{1,0:T(8,128)(2,1)S(1)}, bf16[16,2048]{1,0:T(8,128)(2,1)}, u32[]{:S(2)}) copy-start(bf16[16,2048]{1,0:T(8,128)(2,1)} %param.10) | copy-start | bytes 196612
  253.4 17.9 %all-to-all-start.2 = ((bf16[2,8,4,2048]{3,2,0,1:T(4,128)(2,1)}), bf16[2,8,4,2048]{3,2,0,1:T(4,128)(2,1)S(1)}, u32[]{:S(2)}, u32[]{:S(2)}) async-start(bf16[2,8,4,2048]{3,2,0,1:T(4,128)(2,1)} %copy.61), calls=%async_computation.3 | async-start | bytes 524288 | tf_op jit(solution)/shard_map/all_to_all | solution.py:80
Sparse Core Ops, SparseCore 0:
  34.5 71.6 all-gather.1
  130.5 115.4 reduce-scatter.1
where the time goes:
time: 318 us; the launch traced here: 317 us
  waiting for transfers between devices  194 us (61%)
  blocking collectives  68.7 us (22%)
  matrix products  25.9 us (8%)
  between operations  14.2 us (4%)
  starting transfers between devices  6.86 us (2%)
  local copies, waits for them, and re-layouts  5.59 us (2%)
    reduce_scatter x1, waiting for transfers between devices, per_device(): lax.psum_scatter(jnp.dot(hidden, down_w, preferred_element_type=jnp.float...  111 us
    all_gather x1, waiting for transfers between devices, per_device(): every_row = lax.all_gather(whole, DP, axis=0, tiled=True).reshape(-1, D)  71.8 us
    psum x4, blocking collectives, one_axis_at_a_time(): shard = lax.psum(shard, axis)  37.2 us
    all_to_all x1, blocking collectives, per_device(): lax.all_to_all(outgoing, 'expert', split_axis=1, concat_axis=1, tiled=True)  19.3 us
    dot_general x1, matrix products, per_device(): jnp.dot(hidden, down_w, preferred_element_type=jnp.float32)  16.5 us
    all_to_all x1, waiting for transfers between devices, per_device(): lax.all_to_all(results, 'expert', split_axis=1, concat_axis=1, tiled=True)  10.7 us
    dot_general x1, matrix products, per_device(): gate = jnp.dot(every_row, gate_w, preferred_element_type=jnp.float32)  7.52 us
    all_to_all x1, starting transfers between devices, per_device(): lax.all_to_all(results, 'expert', split_axis=1, concat_axis=1, tiled=True)  6.78 us
  transfers between devices with their start and end apart: 3, of which 3 were waited for; matrix products, arithmetic and copies ran while one was open for 0% of the time, Pallas kernels for 0%

commit v1 on v0

--- a/solution.py
+++ b/solution.py
@@ -77,7 +77,10 @@
     results = summed.astype(jnp.bfloat16).reshape(
         tensor_count, experts, half_cap, D // tensor_count
     )
-    returned = lax.all_to_all(results, "expert", split_axis=1, concat_axis=1, tiled=True)
+    devices = lax.axis_size("expert")
+    blocks = jnp.stack(jnp.split(results, devices, axis=1), axis=0)
+    blocks = lax.all_to_all(blocks, "expert", split_axis=0, concat_axis=0)
+    returned = jnp.concatenate(blocks, axis=1)
     weights = jnp.einsum("rtk,tk->tr", placing.astype(jnp.float32), gates)
     flat_back = returned.reshape(slot_rows, -1).astype(jnp.float32)
     mixed = jnp.dot(weights, flat_back, precision=lax.Precision.HIGHEST).astype(jnp.bfloat16)

time: 318 us -> 322 us (1.013)
  local copies, waits for them, and re-layouts: 5.59 us -> 9.71 us
    unnamed x15 -> x22, local copies, waits for them, and re-layouts: 1.4 us -> 5.7 us
where the time goes in v1:
time: 322 us; the launch traced here: 321 us
  waiting for transfers between devices  194 us (60%)
  blocking collectives  68.7 us (21%)
  matrix products  25.9 us (8%)
  between operations  14.2 us (4%)
  local copies, waits for them, and re-layouts  9.71 us (3%)
  starting transfers between devices  6.86 us (2%)
    reduce_scatter x1, waiting for transfers between devices, per_device(): lax.psum_scatter(jnp.dot(hidden, down_w, preferred_element_type=jnp.float...  111 us
    all_gather x1, waiting for transfers between devices, per_device(): every_row = lax.all_gather(whole, DP, axis=0, tiled=True).reshape(-1, D)  71.8 us
    psum x4, blocking collectives, one_axis_at_a_time(): shard = lax.psum(shard, axis)  37.2 us
    all_to_all x1, blocking collectives, per_device(): lax.all_to_all(outgoing, 'expert', split_axis=1, concat_axis=1, tiled=True)  19.3 us
    dot_general x1, matrix products, per_device(): jnp.dot(hidden, down_w, preferred_element_type=jnp.float32)  16.5 us
    all_to_all x1, waiting for transfers between devices, per_device(): blocks = lax.all_to_all(blocks, 'expert', split_axis=0, concat_axis=0)  10.7 us
    dot_general x1, matrix products, per_device(): gate = jnp.dot(every_row, gate_w, preferred_element_type=jnp.float32)  7.52 us
    all_to_all x1, starting transfers between devices, per_device(): blocks = lax.all_to_all(blocks, 'expert', split_axis=0, concat_axis=0)  6.78 us
  transfers between devices with their start and end apart: 3, of which 3 were waited for; matrix products, arithmetic and copies ran while one was open for 0% of the time, Pallas kernels for 0%

profile of v1, /device:TPU:1, one launch (start us, length us, event | category | flops | bytes accessed | tf_op | source)
XLA Modules:
  0.0 321.2 jit_solution(4121336262141172511)
XLA Ops:
  7.2 0.8 copy.101
  8.6 0.7 fusion.30
  9.4 0.3 convolution_convert_fusion
  9.8 19.3 %all_to_all.15 = bf16[2,8,4,2048]{3,2,0,1:T(4,128)(2,1)S(1)} all-to-all(bf16[2,8,4,2048]{3,2,0,1:T(4,128)(2,1)S(1)} %copy.106), channel_id=1, replica_groups=mesh['dp_0'=4,'dp_1'=4,'expert'=8,'tensor'=2] {'expert'}, dimensions={1} | all-to-all | bytes 524288 | tf_op jit(solution)/shard_map/all_to_all | solution.py:60
  29.2 4.1 %all_gather.6 = bf16[2,8,4,4096]{3,2,0,1:T(4,128)(2,1)S(1)} all-gather(bf16[2,8,4,2048]{3,2,0,1:T(4,128)(2,1)S(1)} %all_to_all.15), channel_id=1, replica_groups=mesh['dp_0'=4,'dp_1'=4,'expert'=8,'tensor'=2] {'tensor'}, dimensions={3}, use_global_device_ids=true | all-gather | bytes 786432 | tf_op jit(solution)/shard_map/all_gather | solution.py:61
  33.3 0.2 copy.107
  33.5 0.9 reshape.109
  34.5 71.8 %all-gather.2.cloned.1.call-done = bf16[16,64,4096]{2,1,0:T(8,128)(2,1)} async-done(((bf16[1,64,4096]{2,1,0:T(8,128)(2,1)}), bf16[16,64,4096]{2,1,0:T(8,128)(2,1)}) %all-gather.2.cloned.1.call-update) | async-done | bytes 8388624 | tf_op jit(solution)/shard_map/all_gather | solution.py:63
  106.3 7.5 %fusion.4 = f32[1024,448]{0,1:T(8,128)S(1)} fusion(bf16[1024,4096]{1,0:T(8,128)(2,1)} %bitcast.95, bf16[1,4096,448]{1,2,0:T(8,128)(2,1)} %param.12), kind=kOutput, calls=%fused_computation.4 | convolution fusion | flops 3758096384 | bytes 13893632 | tf_op jit(solution)/shard_map/dot_general | solution.py:67
  113.8 16.5 %fusion = f32[1024,4096]{1,0:T(8,128)} fusion(bf16[1,448,4096]{2,1,0:T(8,128)(2,1)} %param.14, f32[1024,448]{0,1:T(8,128)S(1)} %fusion.4, bf16[1024,4096]{1,0:T(8,128)(2,1)} %bitcast.96, bf16[1,4096,448]{1,2,0:T(8,128)(2,1)} %param.13), kind=kOutput, calls=%fused_computation | convolution fusion | flops 7518945280 | bytes 34340864 | tf_op jit(solution)/shard_map/dot_general | solution.py:71
  130.4 0.6 copy-done.4
  131.4 3.0 psum.35
  134.7 111.2 %reduce-scatter.2.cloned.1.call-done = f32[64,4096]{1,0:T(8,128)} async-done(((f32[1024,4096]{1,0:T(8,128)}), f32[64,4096]{1,0:T(8,128)}) %reduce-scatter.2.cloned.1.call-update) | async-done | bytes 1048592 | tf_op jit(solution)/shard_map/reduce_scatter | solution.py:70
  246.0 1.3 copy.132
  247.3 5.1 %all_to_all.16 = f32[2,64,2048]{2,1,0:T(8,128)S(1)} all-to-all(f32[2,64,2048]{2,1,0:T(8,128)S(1)} %bitcast.90), channel_id=1, replica_groups=mesh['dp_0'=4,'dp_1'=4,'expert'=8,'tensor'=2] {'tensor'}, dimensions={0} | all-to-all | bytes 2097152 | tf_op jit(solution)/shard_map/all_to_all | solution.py:23
  252.6 0.6 fusion.18
  253.2 0.6 fusion.17
  253.8 0.6 fusion.16
  254.4 0.6 fusion.15
  255.0 0.6 fusion.14
  255.7 0.6 fusion.13
  256.3 0.6 fusion.12
  256.9 0.6 fusion.11
  257.5 6.8 %all-to-all-start.2 = ((bf16[8,2,1,4,2048]{4,3,1,2,0:T(4,128)(2,1)}), bf16[8,2,1,4,2048]{4,3,1,2,0:T(4,128)(2,1)S(1)}, u32[]{:S(2)}, u32[]{:S(2)}) async-start(bf16[8,2,1,4,2048]{4,3,1,2,0:T(4,128)(2,1)} %fusion.11), calls=%async_computation.3 | async-start | bytes 524288 | tf_op jit(solution)/shard_map/all_to_all | solution.py:82
  264.4 0.2 fusion.22
  264.7 10.7 %all-to-all-done.2 = bf16[8,2,1,4,2048]{4,3,1,2,0:T(4,128)(2,1)S(1)} async-done(((bf16[8,2,1,4,2048]{4,3,1,2,0:T(4,128)(2,1)}), bf16[8,2,1,4,2048]{4,3,1,2,0:T(4,128)(2,1)S(1)}, u32[]{:S(2)}, u32[]{:S(2)}) %all-to-all-start.2) | async-done | bytes 262176 | tf_op jit(solution)/shard_map/all_to_all | solution.py:82
  275.6 1.0 multiply_reduce_fusion
  276.7 8.0 %psum.36 = f32[16]{0:T(128)S(1)} all-reduce(f32[16]{0:T(128)S(1)} %convolution_bitcast_fusion), channel_id=1, replica_groups=mesh['dp_0'=4,'dp_1'=4,'expert'=8,'tensor'=2] {'dp_0'}, use_global_device_ids=true, to_apply=%region_10.11 | all-reduce | flops 16 | bytes 128 | tf_op jit(solution)/shard_map/psum | solution.py:29
  284.6 6.7 %psum.37 = f32[16]{0:T(128)S(1)} all-reduce(f32[16]{0:T(128)S(1)} %psum.36), channel_id=1, replica_groups=mesh['dp_0'=4,'dp_1'=4,'expert'=8,'tensor'=2] {'dp_1'}, use_global_device_ids=true, to_apply=%region_11.12 | all-reduce | flops 16 | bytes 128 | tf_op jit(solution)/shard_map/psum | solution.py:29
  291.3 10.7 %psum.38 = f32[16]{0:T(128)S(1)} all-reduce(f32[16]{0:T(128)S(1)} %psum.37), channel_id=1, replica_groups=mesh['dp_0'=4,'dp_1'=4,'expert'=8,'tensor'=2] {'expert'}, use_global_device_ids=true, to_apply=%region_12.13 | all-reduce | flops 16 | bytes 128 | tf_op jit(solution)/shard_map/psum | solution.py:29
  302.0 11.9 %psum.39 = f32[16]{0:T(128)S(1)} all-reduce(f32[16]{0:T(128)S(1)} %psum.38), channel_id=1, replica_groups=mesh['dp_0'=4,'dp_1'=4,'expert'=8,'tensor'=2] {'tensor'}, use_global_device_ids=true, to_apply=%region_13.14 | all-reduce | flops 16 | bytes 128 | tf_op jit(solution)/shard_map/psum | solution.py:29
  313.9 0.5 convert_divide_fusion
  (44 shorter events, 2.5 us)
Async XLA Ops:
  7.2 2.2 copy-start
  7.2 99.1 %all-gather.2.cloned.1.call-start = ((), (), s32[]{:S(2)}) async-start(), calls=%async_computation.4 | async-start | bytes 8912896 | tf_op jit(solution)/shard_map/all_gather | solution.py:63
  34.4 211.6 %reduce-scatter.2.cloned.1.call-start = ((), (), s32[]{:S(2)}) async-start(), calls=%async_computation.5 | async-start | bytes 17825792 | tf_op jit(solution)/shard_map/reduce_scatter | solution.py:70
  130.3 0.7 copy-start.4
  130.3 1.0 copy-start.2
  130.3 4.1 %copy-start.5 = (s32[64]{0:T(128)S(1)}, s32[64]{0:T(128)}, u32[]{:S(2)}) copy-start(s32[64]{0:T(128)} %param.17) | copy-start | bytes 772
  130.3 4.2 %copy-start.3 = (s32[16,2]{0,1:T(2,128)S(1)}, s32[16,2]{0,1:T(2,128)}, u32[]{:S(2)}) copy-start(s32[16,2]{0,1:T(2,128)} %param.15) | copy-start | bytes 388
  134.5 179.4 %copy-start.6 = (s32[16]{0:T(128)}, s32[16]{0:T(128)S(1)}, u32[]{:S(2)}) copy-start(s32[16]{0:T(128)S(1)} %select_reduce_fusion.1) | copy-start | bytes 196
  246.0 29.6 %copy-start.1 = (bf16[16,2048]{1,0:T(8,128)(2,1)S(1)}, bf16[16,2048]{1,0:T(8,128)(2,1)}, u32[]{:S(2)}) copy-start(bf16[16,2048]{1,0:T(8,128)(2,1)} %param.10) | copy-start | bytes 196612
  257.5 17.9 %all-to-all-start.2 = ((bf16[8,2,1,4,2048]{4,3,1,2,0:T(4,128)(2,1)}), bf16[8,2,1,4,2048]{4,3,1,2,0:T(4,128)(2,1)S(1)}, u32[]{:S(2)}, u32[]{:S(2)}) async-start(bf16[8,2,1,4,2048]{4,3,1,2,0:T(4,128)(2,1)} %fusion.11), calls=%async_computation.3 | async-start | bytes 524288 | tf_op jit(solution)/shard_map/all_to_all | solution.py:82
Sparse Core Ops, SparseCore 0:
  34.5 71.6 all-gather.1
  130.5 115.4 reduce-scatter.1
